TPU v7x, 32 devices: a whole 2x2x4 slice. The times are simulated.
32 devices in a mesh: tissue: 2 (over core), row: 4 (over y, x), col: 4 (over z).
Axes of the slice: x: 2, y: 2, z: 4, core: 2. Of those that a mesh axis runs over, the one named last changes fastest.
Arguments:
- expr: float32 [1200, 16384], P(('tissue', 'row'), 'col'), parts along dimension 0, may hold values from -48 to 88
- win_genes: int32 [256], replicated, may hold values from 0 to 16383, as said below
Outputs:
- margin: float32 [512, 16384], P(('tissue', 'row'), 'col'), parts along dimension 0
- degree: float32 [32768], P(('tissue', 'col')), parts along dimension 0
There are 2 independent parts, one for each index of `tissue`. A program takes and returns all parts, laid end to end along the dimension named above; an argument that names none is the same for every part. Nothing has to cross between parts.
Inputs may be any that keep to these rules, and one draw needn't show every extreme that they name: `win_genes`: 256 distinct gene numbers.
All inputs are finite; a program needn't handle non-finite values.
Results may differ from a plain program's by a relative error of at most 0.00077.
Values may be sent and summed in bfloat16 or wider, within the bound.
A program may use at most 128 MiB of HBM per device.

v0:
```python
import jax
import jax.numpy as jnp
from jax import lax
from jax.sharding import PartitionSpec as P


def power_eight(corr):
    half = (1.0 + corr) * 0.5
    half = half * half
    half = half * half
    return half * half


def inner_first(left, right):
    return lax.dot_general(
        left, right, (((0,), (0,)), ((), ())), preferred_element_type=jnp.float32
    )


def body(expr, win_genes):
    n_row = lax.axis_size("row")
    samples_all = expr.shape[0] * n_row
    totals = lax.psum(jnp.sum(expr, axis=0), "row")
    centered = expr - totals / samples_all
    squares = lax.psum(jnp.sum(centered * centered, axis=0), "row")
    z = (centered / jnp.sqrt(squares + 1e-06)).astype(jnp.bfloat16)
    zcol = lax.all_gather(z, "row", axis=0, tiled=True)
    width = zcol.shape[1]
    slab = width // n_row
    row_id = lax.axis_index("row")
    col_id = lax.axis_index("col")
    zpiece = lax.dynamic_slice_in_dim(zcol, row_id * slab, slab, 1)
    zrows = lax.all_gather(zpiece, "col", axis=1, tiled=True)
    adj = power_eight(inner_first(zrows, zcol)).astype(jnp.bfloat16)
    local_rows = jnp.arange(zrows.shape[1], dtype=jnp.int32)
    genes_i = local_rows // slab * width + row_id * slab + local_rows % slab
    genes_j = col_id * width + jnp.arange(width, dtype=jnp.int32)
    keep = genes_i[:, None] != genes_j[None, :]
    partial_degree = jnp.sum(jnp.where(keep, adj.astype(jnp.float32), jnp.float32(0.0)), axis=0)
    degree = lax.psum(partial_degree, "row")
    offsets = win_genes - col_id * width
    inside = (offsets >= 0) & (offsets < width)
    clipped = jnp.clip(offsets, 0, width - 1)
    picked = jnp.take(zcol, clipped, axis=1)
    terms = jnp.where(inside[None, :], picked, jnp.zeros((), jnp.bfloat16))
    zwin = lax.psum(terms, "col").astype(jnp.float32).astype(jnp.bfloat16)
    panel = power_eight(inner_first(zrows, zwin)).astype(jnp.bfloat16)
    margin = lax.psum_scatter(inner_first(panel, adj), "row", scatter_dimension=0, tiled=True)
    return (margin, degree)


def solution(mesh):
    in_specs = (P(("tissue", "row"), "col"), P())
    out_specs = (P(("tissue", "row"), "col"), P(("tissue", "col")))
    return jax.shard_map(body, mesh=mesh, in_specs=in_specs, out_specs=out_specs, check_vma=False)
```

profile of v0, /device:TPU:0, one launch (start us, length us, event | category | flops | bytes accessed | tf_op | source)
XLA Modules:
  0.0 335.1 jit_solution(13726724207227180818)
XLA Ops:
  7.2 0.0 copy-start
  7.2 0.0 all-gather.6.cloned.1.call-start
  7.2 2.0 reduce_sum.27
  9.2 17.5 %psum.28 = f32[4096]{0:T(1024)S(1)} all-reduce(f32[4096]{0:T(1024)S(1)} %reduce_sum.27), channel_id=1, replica_groups=mesh['tissue'=2,'row'=4,'col'=4] {'row'}, use_global_device_ids=true, to_apply=%region_1.0 | all-reduce | flops 4096 | bytes 32768 | tf_op jit(solution)/shard_map/psum | solution.py:23
  26.7 2.0 multiply_reduce_fusion
  28.7 13.7 %psum.29 = f32[4096]{0:T(1024)S(1)} all-reduce(f32[4096]{0:T(1024)S(1)} %multiply_reduce_fusion), channel_id=1, replica_groups=mesh['tissue'=2,'row'=4,'col'=4] {'row'}, use_global_device_ids=true, to_apply=%region_3.0 | all-reduce | flops 4096 | bytes 32768 | tf_op jit(solution)/shard_map/psum | solution.py:25
  42.5 0.0 copy-done
  42.5 1.3 fusion.5
  43.8 0.0 all-gather.6.cloned.1.call-update
  43.8 0.0 all-gather.4.cloned.1.call-start
  43.9 0.0 copy-start.1
  43.9 59.8 %all-gather.6.cloned.1.call-done = bf16[4,150,4096]{2,1,0:T(8,128)(2,1)} async-done(((bf16[1,150,4096]{2,1,0:T(8,128)(2,1)}), bf16[4,150,4096]{2,1,0:T(8,128)(2,1)}) %all-gather.6.cloned.1.call-update) | async-done | bytes 4915216 | tf_op jit(solution)/shard_map/all_gather | solution.py:27
  103.7 6.0 %reshape.49 = bf16[600,4096]{1,0:T(8,128)(2,1)} reshape(bf16[4,150,4096]{2,1,0:T(8,128)(2,1)} %all-gather.6.cloned.1.call-done) | data formatting | bytes 9830400
  109.7 2.4 constant_dynamic-slice_fusion
  112.1 0.0 all-gather.4.cloned.1.call-update
  112.2 0.0 all-reduce.2.cloned.1.call-start
  112.2 0.0 copy-done.1
  112.3 7.9 %copy.6 = bf16[600,4096]{0,1:T(8,128)(2,1)} copy(bf16[600,4096]{1,0:T(8,128)(2,1)} %reshape.49) | data formatting | bytes 9830400
  120.1 4.9 %gather_fusion = bf16[256,600]{1,0:T(8,128)(2,1)S(1)} fusion(bf16[600,4096]{0,1:T(8,128)(2,1)} %copy.6, s32[1024]{0:T(1024)S(1)} %pad_clamp_fusion), kind=kCustom, calls=%fused_computation | custom fusion | bytes 615424 | tf_op jit(solution)/shard_map/jit(_take)/gather | solution.py:44
  125.0 0.9 select_bitcast_fusion
  125.9 0.0 all-reduce.2.cloned.1.call-update
  125.9 0.2 reduce-scatter.2.cloned.1.call-start
  126.1 78.8 %all-gather.4.cloned.1.call-done = bf16[600,4096]{1,0:T(8,128)(2,1)} async-done(((bf16[600,1024]{1,0:T(8,128)(2,1)}), bf16[600,4096]{1,0:T(8,128)(2,1)}) %all-gather.4.cloned.1.call-update) | async-done | bytes 4915216 | tf_op jit(solution)/shard_map/all_gather | solution.py:33
  204.9 45.1 %select_reduce_fusion = (f32[4096]{0:T(1024)S(1)}, bf16[4096,4096]{1,0:T(8,128)(2,1)}) fusion(s32[4096]{0:T(1024)S(1)} %get-tuple-element.8, s32[4096]{0:T(1024)S(1)} %get-tuple-element.7, bf16[600,4096]{1,0:T(8,128)(2,1)} %all-gather.4.cloned.1.call-done, bf16[600,4096]{1,0:T(8,128)(2,1)} %reshape.49), kind=kOutput, calls=%fused_computation.1 | convolution fusion | flops 20300427264 | bytes 43433984 | tf_op jit(solution)/shard_map/dot_general | solution.py:15
  250.1 0.0 all-reduce.2.cloned.1.call-done
  250.1 27.1 %fusion.6 = f32[256,4096]{1,0:T(8,128)} fusion(bf16[4096,4096]{1,0:T(8,128)(2,1)} %get-tuple-element.6, bf16[600,4096]{1,0:T(8,128)(2,1)} %all-gather.4.cloned.1.call-done, bf16[600,256]{0,1:T(8,128)(2,1)} %all-reduce.2.cloned.1.call-done), kind=kOutput, calls=%fused_computation.12 | convolution fusion | flops 9854517248 | bytes 42971136 | tf_op jit(solution)/shard_map/dot_general | solution.py:15
  277.2 0.0 reduce-scatter.2.cloned.1.call-update
  277.2 17.3 %psum.31 = f32[4096]{0:T(1024)} all-reduce(f32[4096]{0:T(1024)S(1)} %get-tuple-element.5), channel_id=1, replica_groups=mesh['tissue'=2,'row'=4,'col'=4] {'row'}, use_global_device_ids=true, to_apply=%region_7.8 | all-reduce | flops 4096 | bytes 32768 | tf_op jit(solution)/shard_map/psum | solution.py:40
  294.5 34.0 %reduce-scatter.2.cloned.1.call-done = f32[64,4096]{1,0:T(8,128)} async-done(((f32[256,4096]{1,0:T(8,128)}), f32[64,4096]{1,0:T(8,128)}) %reduce-scatter.2.cloned.1.call-update) | async-done | bytes 1048592 | tf_op jit(solution)/shard_map/reduce_scatter | solution.py:48
  (5 shorter events, 0.1 us)
Async XLA Ops:
  7.2 35.3 %copy-start = (f32[150,4096]{1,0:T(8,128)S(1)}, f32[150,4096]{1,0:T(8,128)}, u32[]{:S(2)}) copy-start(f32[150,4096]{1,0:T(8,128)} %param.2) | copy-start | bytes 7372804
  7.2 96.5 %all-gather.6.cloned.1.call-start = ((), (), s32[]{:S(2)}) async-start(), calls=%async_computation.4 | async-start | bytes 6225920 | tf_op jit(solution)/shard_map/all_gather | solution.py:27
  43.8 161.1 %all-gather.4.cloned.1.call-start = ((), (), s32[]{:S(2)}) async-start(), calls=%async_computation.1 | async-start | bytes 6144000 | tf_op jit(solution)/shard_map/all_gather | solution.py:33
  43.9 68.3 %copy-start.1 = (s32[256]{0:T(256)S(1)}, s32[256]{0:T(256)}, u32[]{:S(2)}) copy-start(s32[256]{0:T(256)} %param.3) | copy-start | bytes 3076
  112.2 137.9 %all-reduce.2.cloned.1.call-start = ((), (), s32[]{:S(2)}) async-start(), calls=%async_computation.2 | async-start | bytes 655360 | tf_op jit(solution)/shard_map/psum | solution.py:46
  125.9 202.6 %reduce-scatter.2.cloned.1.call-start = ((), (), s32[]{:S(2)}) async-start(), calls=%async_computation.3 | async-start | bytes 5242880 | tf_op jit(solution)/shard_map/reduce_scatter | solution.py:48
Sparse Core Ops, SparseCore 0:
  44.0 59.7 all-gather.5
  112.3 92.6 all-gather.3
  207.9 34.8 all-reduce.1
  277.3 51.1 reduce-scatter.1
where the time goes:
time: 336 us; the launch traced here: 335 us
  waiting for transfers between devices  173 us (51%)
  matrix products  72.2 us (21%)
  blocking collectives  48.5 us (14%)
  local copies, waits for them, and re-layouts  21.1 us (6%)
  between operations  13.8 us (4%)
  other arithmetic  6.23 us (2%)
    all_gather x1, waiting for transfers between devices, body(): zrows = lax.all_gather(zpiece, 'col', axis=1, tiled=True)  78.8 us
    dot_general x2, matrix products, inner_first(): lax.dot_general(left, right, (((0,), (0,)), ((), ())), preferred_element_...  72.2 us
    all_gather x1, waiting for transfers between devices, body(): zcol = lax.all_gather(z, 'row', axis=0, tiled=True)  59.8 us
    reduce_scatter x1, waiting for transfers between devices, body(): lax.psum_scatter(inner_first(panel, adj), 'row', scatter_dimension=0, til...  34 us
    psum x1, blocking collectives, body(): totals = lax.psum(jnp.sum(expr, axis=0), 'row')  17.5 us
    psum x1, blocking collectives, body(): degree = lax.psum(partial_degree, 'row')  17.3 us
    unnamed x6, local copies, waits for them, and re-layouts  13.8 us
    psum x1, blocking collectives, body(): squares = lax.psum(jnp.sum(centered * centered, axis=0), 'row')  13.7 us
  transfers between devices with their start and end apart: 4, of which 3 were waited for; matrix products, arithmetic and copies ran while one was open for 18% of the time, Pallas kernels for 0%

commit v1 on v0

--- a/solution.py
+++ b/solution.py
@@ -24,7 +24,12 @@
     centered = expr - totals / samples_all
     squares = lax.psum(jnp.sum(centered * centered, axis=0), "row")
     z = (centered / jnp.sqrt(squares + 1e-06)).astype(jnp.bfloat16)
-    zcol = lax.all_gather(z, "row", axis=0, tiled=True)
+    ring = [z]
+    for hop in range(3):
+        ring.append(lax.ppermute(ring[-1], "row", [(dev, (dev + 1) % 4) for dev in range(4)]))
+    zcol = jnp.roll(
+        jnp.concatenate(ring[::-1], axis=0), (lax.axis_index("row") + 1) * ring[0].shape[0], axis=0
+    )
     width = zcol.shape[1]
     slab = width // n_row
     row_id = lax.axis_index("row")

time: 336 us -> 403 us (1.20)
  local copies, waits for them, and re-layouts: 21.1 us -> 76.5 us
  waiting for transfers between devices: 173 us -> 181 us
    ppermute x0 -> x3, waiting for transfers between devices: none -> 74.5 us  [body(): lax.ppermute(ring[-1], 'row', [(dev, (dev + 1) % 4) for dev in range(4)])]
    all_gather x1 -> x0, waiting for transfers between devices: 59.8 us -> none  [body(): zcol = lax.all_gather(z, 'row', axis=0, tiled=True)]
    concatenate x0 -> x1, local copies, waits for them, and re-layouts: none -> 54 us  [body(): jnp.roll(jnp.concatenate(ring[::-1], axis=0), (lax.axis_index('row') + 1)...]
    dynamic_slice x0 -> x2, local copies, waits for them, and re-layouts: none -> 13.9 us  [body(): jnp.roll(jnp.concatenate(ring[::-1], axis=0), (lax.axis_index('row') + 1)...]
    unnamed x6, local copies, waits for them, and re-layouts: 13.8 us -> 1.04 us
    all_gather x1, waiting for transfers between devices: 78.8 us -> 72.9 us  [body(): zrows = lax.all_gather(zpiece, 'col', axis=1, tiled=True)]
  transfers between devices with their start and end apart: 4 -> 6, of which waited for: 3 -> 5; matrix products, arithmetic and copies ran while one was open for 18% -> 16% of each run, Pallas kernels for 0% -> 0%
where the time goes in v1:
time: 403 us; the launch traced here: 400 us
  waiting for transfers between devices  181 us (45%)
  local copies, waits for them, and re-layouts  76.5 us (19%)
  matrix products  72.3 us (18%)
  blocking collectives  48.7 us (12%)
  between operations  13.8 us (3%)
  other arithmetic  5.17 us (1%)
    ppermute x3, waiting for transfers between devices, body(): lax.ppermute(ring[-1], 'row', [(dev, (dev + 1) % 4) for dev in range(4)])  74.5 us
    all_gather x1, waiting for transfers between devices, body(): zrows = lax.all_gather(zpiece, 'col', axis=1, tiled=True)  72.9 us
    dot_general x2, matrix products, inner_first(): lax.dot_general(left, right, (((0,), (0,)), ((), ())), preferred_element_...  72.3 us
    concatenate x1, local copies, waits for them, and re-layouts, body(): jnp.roll(jnp.concatenate(ring[::-1], axis=0), (lax.axis_index('row') + 1)...  54 us
    reduce_scatter x1, waiting for transfers between devices, body(): lax.psum_scatter(inner_first(panel, adj), 'row', scatter_dimension=0, til...  34.1 us
    psum x1, blocking collectives, body(): totals = lax.psum(jnp.sum(expr, axis=0), 'row')  17.5 us
    psum x1, blocking collectives, body(): degree = lax.psum(partial_degree, 'row')  17.3 us
    dynamic_slice x2, local copies, waits for them, and re-layouts, body(): jnp.roll(jnp.concatenate(ring[::-1], axis=0), (lax.axis_index('row') + 1)...  13.9 us
  transfers between devices with their start and end apart: 6, of which 5 were waited for; matrix products, arithmetic and copies ran while one was open for 16% of the time, Pallas kernels for 0%

profile of v1, /device:TPU:0, one launch (start us, length us, event | category | flops | bytes accessed | tf_op | source)
XLA Modules:
  0.0 399.9 jit_solution(5904434342051507177)
XLA Ops:
  7.2 0.0 copy-start
  7.2 0.0 all-gather.2.cloned.1.call-start
  7.2 2.0 reduce_sum.27
  9.2 17.5 %psum.28 = f32[4096]{0:T(1024)S(1)} all-reduce(f32[4096]{0:T(1024)S(1)} %reduce_sum.27), channel_id=1, replica_groups=mesh['tissue'=2,'row'=4,'col'=4] {'row'}, use_global_device_ids=true, to_apply=%region_1.0 | all-reduce | flops 4096 | bytes 32768 | tf_op jit(solution)/shard_map/psum | solution.py:23
  26.7 2.0 multiply_reduce_fusion
  28.7 13.9 %psum.29 = f32[4096]{0:T(1024)S(1)} all-reduce(f32[4096]{0:T(1024)S(1)} %multiply_reduce_fusion), channel_id=1, replica_groups=mesh['tissue'=2,'row'=4,'col'=4] {'row'}, use_global_device_ids=true, to_apply=%region_3.0 | all-reduce | flops 4096 | bytes 32768 | tf_op jit(solution)/shard_map/psum | solution.py:25
  42.6 0.0 copy-done
  42.6 0.3 divide_convert_fusion
  42.9 0.0 copy-start.1
  42.9 1.0 copy-done.1
  43.9 1.0 collective-permute-start
  44.9 26.6 %collective-permute-done = bf16[150,4096]{1,0:T(8,128)(2,1)S(1)} collective-permute-done((bf16[150,4096]{1,0:T(8,128)(2,1)S(1)}, bf16[150,4096]{1,0:T(8,128)(2,1)S(1)}, u32[]{:S(2)}, u32[]{:S(2)}) %collective-permute-start) | collective-permute-done | bytes 1228832 | tf_op jit(solution)/shard_map/ppermute | solution.py:29
  71.5 0.3 collective-permute-start.1
  71.8 27.2 %collective-permute-done.1 = bf16[150,4096]{1,0:T(8,128)(2,1)S(1)} collective-permute-done((bf16[150,4096]{1,0:T(8,128)(2,1)S(1)}, bf16[150,4096]{1,0:T(8,128)(2,1)S(1)}, u32[]{:S(2)}, u32[]{:S(2)}) %collective-permute-start.1) | collective-permute-done | bytes 1228832 | tf_op jit(solution)/shard_map/ppermute | solution.py:29
  99.0 0.3 collective-permute-start.2
  99.3 0.0 copy-start.2
  99.3 20.7 %collective-permute-done.2 = bf16[150,4096]{1,0:T(8,128)(2,1)} collective-permute-done((bf16[150,4096]{1,0:T(8,128)(2,1)S(1)}, bf16[150,4096]{1,0:T(8,128)(2,1)}, u32[]{:S(2)}, u32[]{:S(2)}) %collective-permute-start.2) | collective-permute-done | bytes 1228832 | tf_op jit(solution)/shard_map/ppermute | solution.py:29
  120.1 54.0 %concatenate.6 = bf16[1200,4096]{1,0:T(8,128)(2,1)} concatenate(bf16[150,4096]{1,0:T(8,128)(2,1)} %collective-permute-done.2, bf16[150,4096]{1,0:T(8,128)(2,1)S(1)} %collective-permute-done.1, bf16[150,4096]{1,0:T(8,128)(2,1)S(1)} %collective-permute-done, bf16[150,4096]{1,0:T(8,128)(2,1)} %copy-done.1, bf16[150,4096]{1,0:T(8,128)(2,1)} %collective-permute-done.2, ...), dimensions={0} | concatenate | bytes 19660800 | tf_op jit(solution)/shard_map/jit(_roll_dynamic)/concatenate | solution.py:30
  174.1 3.1 dynamic_slice.7
  177.2 0.0 all-gather.2.cloned.1.call-update
  177.2 0.0 all-reduce.2.cloned.1.call-start
  177.2 0.0 copy-done.2
  177.3 6.0 %constant_dynamic-slice_fusion = bf16[600,4096]{1,0:T(8,128)(2,1)} fusion(bf16[1200,4096]{1,0:T(8,128)(2,1)} %concatenate.6, s32[]{:T(128)S(6)} %select_n.57), kind=kLoop, calls=%fused_computation.34 | loop fusion | bytes 9830404 | tf_op jit(solution)/shard_map/jit(_roll_dynamic)/dynamic_slice | solution.py:30
  183.3 7.9 %copy.13 = bf16[600,4096]{0,1:T(8,128)(2,1)} copy(bf16[600,4096]{1,0:T(8,128)(2,1)} %constant_dynamic-slice_fusion) | data formatting | bytes 9830400 | tf_op jit(solution)/shard_map/jit(_roll_dynamic)/dynamic_slice | solution.py:30
  191.2 4.5 %gather_fusion = bf16[256,600]{1,0:T(8,128)(2,1)S(1)} fusion(bf16[600,4096]{0,1:T(8,128)(2,1)} %copy.13, s32[1024]{0:T(1024)S(1)} %pad_clamp_fusion), kind=kCustom, calls=%fused_computation | custom fusion | bytes 615424 | tf_op jit(solution)/shard_map/jit(_take)/gather | solution.py:49
  195.7 0.9 select_bitcast_fusion
  196.6 0.0 all-reduce.2.cloned.1.call-update
  196.6 0.2 reduce-scatter.2.cloned.1.call-start
  196.8 72.9 %all-gather.2.cloned.1.call-done = bf16[600,4096]{1,0:T(8,128)(2,1)} async-done(((bf16[600,1024]{1,0:T(8,128)(2,1)}), bf16[600,4096]{1,0:T(8,128)(2,1)}) %all-gather.2.cloned.1.call-update) | async-done | bytes 4915216 | tf_op jit(solution)/shard_map/all_gather | solution.py:38
  269.7 45.1 %select_reduce_fusion = (f32[4096]{0:T(1024)S(1)}, bf16[4096,4096]{1,0:T(8,128)(2,1)}) fusion(s32[4096]{0:T(1024)S(1)} %get-tuple-element.8, s32[4096]{0:T(1024)S(1)} %get-tuple-element.7, bf16[600,4096]{1,0:T(8,128)(2,1)} %all-gather.2.cloned.1.call-done, bf16[600,4096]{1,0:T(8,128)(2,1)} %constant_dynamic-slice_fusion), kind=kOutput, calls=%fused_computation.1 | convolution fusion | flops 20300427264 | bytes 43433984 | tf_op jit(solution)/shard_map/dot_general | solution.py:15
  314.8 0.0 all-reduce.2.cloned.1.call-done
  314.8 27.1 %fusion.5 = f32[256,4096]{1,0:T(8,128)} fusion(bf16[4096,4096]{1,0:T(8,128)(2,1)} %get-tuple-element.6, bf16[600,4096]{1,0:T(8,128)(2,1)} %all-gather.2.cloned.1.call-done, bf16[600,256]{0,1:T(8,128)(2,1)} %all-reduce.2.cloned.1.call-done), kind=kOutput, calls=%fused_computation.11 | convolution fusion | flops 9854517248 | bytes 42971136 | tf_op jit(solution)/shard_map/dot_general | solution.py:15
  342.0 0.0 reduce-scatter.2.cloned.1.call-update
  342.0 17.3 %psum.31 = f32[4096]{0:T(1024)} all-reduce(f32[4096]{0:T(1024)S(1)} %get-tuple-element.5), channel_id=1, replica_groups=mesh['tissue'=2,'row'=4,'col'=4] {'row'}, use_global_device_ids=true, to_apply=%region_7.8 | all-reduce | flops 4096 | bytes 32768 | tf_op jit(solution)/shard_map/psum | solution.py:45
  359.3 34.1 %reduce-scatter.2.cloned.1.call-done = f32[64,4096]{1,0:T(8,128)} async-done(((f32[256,4096]{1,0:T(8,128)}), f32[64,4096]{1,0:T(8,128)}) %reduce-scatter.2.cloned.1.call-update) | async-done | bytes 1048592 | tf_op jit(solution)/shard_map/reduce_scatter | solution.py:53
  (5 shorter events, 0.0 us)
Async XLA Ops:
  7.2 35.4 %copy-start = (f32[150,4096]{1,0:T(8,128)S(1)}, f32[150,4096]{1,0:T(8,128)}, u32[]{:S(2)}) copy-start(f32[150,4096]{1,0:T(8,128)} %param.2) | copy-start | bytes 7372804
  7.2 262.5 %all-gather.2.cloned.1.call-start = ((), (), s32[]{:S(2)}) async-start(), calls=%async_computation.1 | async-start | bytes 6144000 | tf_op jit(solution)/shard_map/all_gather | solution.py:38
  42.9 1.0 copy-start.1
  43.9 27.5 %collective-permute-start = (bf16[150,4096]{1,0:T(8,128)(2,1)S(1)}, bf16[150,4096]{1,0:T(8,128)(2,1)S(1)}, u32[]{:S(2)}, u32[]{:S(2)}) collective-permute-start(bf16[150,4096]{1,0:T(8,128)(2,1)S(1)} %divide_convert_fusion), channel_id=1, source_target_pairs={{0,4},{4,8},{8,12},{12,0},{1,5},{5,9},{9,13},{13,1},{2,6},{6,10},{... | collective-permute-start | bytes 3686408 | tf_op jit(solution)/shard_map/ppermute | solution.py:29
  71.5 27.5 %collective-permute-start.1 = (bf16[150,4096]{1,0:T(8,128)(2,1)S(1)}, bf16[150,4096]{1,0:T(8,128)(2,1)S(1)}, u32[]{:S(2)}, u32[]{:S(2)}) collective-permute-start(bf16[150,4096]{1,0:T(8,128)(2,1)S(1)} %collective-permute-done), channel_id=1, source_target_pairs={{0,4},{4,8},{8,12},{12,0},{1,5},{5,9},{9,13},{13,1},{2,6},{6,10},{... | collective-permute-start | bytes 3686408 | tf_op jit(solution)/shard_map/ppermute | solution.py:29
  99.0 21.1 %collective-permute-start.2 = (bf16[150,4096]{1,0:T(8,128)(2,1)S(1)}, bf16[150,4096]{1,0:T(8,128)(2,1)}, u32[]{:S(2)}, u32[]{:S(2)}) collective-permute-start(bf16[150,4096]{1,0:T(8,128)(2,1)S(1)} %collective-permute-done.1), channel_id=1, source_target_pairs={{0,4},{4,8},{8,12},{12,0},{1,5},{5,9},{9,13},{13,1},{2,6},{6,10},{... | collective-permute-start | bytes 3686408 | tf_op jit(solution)/shard_map/ppermute | solution.py:29
  99.3 77.9 %copy-start.2 = (s32[256]{0:T(256)S(1)}, s32[256]{0:T(256)}, u32[]{:S(2)}) copy-start(s32[256]{0:T(256)} %param.3) | copy-start | bytes 3076
  177.2 137.6 %all-reduce.2.cloned.1.call-start = ((), (), s32[]{:S(2)}) async-start(), calls=%async_computation.2 | async-start | bytes 655360 | tf_op jit(solution)/shard_map/psum | solution.py:51
  196.6 196.7 %reduce-scatter.2.cloned.1.call-start = ((), (), s32[]{:S(2)}) async-start(), calls=%async_computation.3 | async-start | bytes 5242880 | tf_op jit(solution)/shard_map/reduce_scatter | solution.py:53
Sparse Core Ops, SparseCore 0:
  177.3 92.3 all-gather.1
  272.6 34.8 all-reduce.1
  342.1 51.1 reduce-scatter.1
